TPU v7x, 32 devices: a whole 2x2x4 slice. The times are simulated.
32 devices in a mesh: head: 2 (over core), seq: 8 (over z, y), mp: 2 (over x).
Axes of the slice: x: 2, y: 2, z: 4, core: 2. Of those that a mesh axis runs over, the one named last changes fastest.
Arguments:
- trunk: bfloat16 [128, 8192], P('seq', 'mp'), may hold values from -6 to 6
- branch: bfloat16 [2, 128, 8192], P('head', 'seq', 'mp'), may hold values from -6 to 6
- unembed: bfloat16 [18432, 8192], P('seq', 'mp'), may hold values from -0.09375 to 0.09375
- targets: int32 [2, 128], P('head'), may hold values from 0 to 18431
- loss_grad: float32 [2, 128], P('head'), may hold values from 0.25 to 4
Outputs:
- d_branch: bfloat16 [2, 128, 8192], P('head', 'seq', 'mp')
- d_trunk: bfloat16 [128, 8192], P('seq', 'mp')
- d_unembed: float32 [18432, 8192], P('seq', 'mp')
All inputs are finite; a program needn't handle non-finite values.
Results may differ from a plain program's by a relative error of at most 0.0051.
Values may be sent and summed in bfloat16 or wider, within the bound.
No kernel may reach another device: no remote copies, remote signals or barrier semaphores. Data moves between devices by JAX's collectives and lax.ppermute only.
A program may use at most 192 MiB of HBM per device.

v0:
```python
import jax
import jax.numpy as jnp
from jax import lax
from jax.sharding import PartitionSpec as P

soft_cap = 30.0


def shards(trunk, branch, unembed, targets, loss_grad):
    block_rows = unembed.shape[0]
    hidden = (trunk.astype(jnp.float32) + branch[0].astype(jnp.float32)).astype(jnp.bfloat16)
    gathered = lax.all_gather(hidden, "seq", axis=0, tiled=True)
    seq_index = lax.axis_index("seq")
    scores = lax.psum(
        lax.dot_general(
            unembed, gathered, (((1,), (1,)), ((), ())), preferred_element_type=jnp.float32
        ),
        "mp",
    )
    first_vocab = seq_index * block_rows
    squashed = jnp.tanh(scores / soft_cap)
    exponent = jnp.exp(soft_cap * squashed)
    totals = lax.psum(jnp.sum(exponent, axis=0), "seq")
    vocab_ids = first_vocab + lax.iota(jnp.int32, scores.shape[0])
    onehot = (vocab_ids[:, None] == targets[0][None, :]).astype(jnp.float32)
    slope = (
        loss_grad[0][None, :] * (exponent / totals[None, :] - onehot) * (1.0 - squashed * squashed)
    )
    grad_logits = slope.astype(jnp.bfloat16)
    weight_grad = jnp.dot(grad_logits, gathered, preferred_element_type=jnp.float32)
    row_grad = lax.psum_scatter(
        lax.dot_general(
            grad_logits, unembed, (((0,), (0,)), ((), ())), preferred_element_type=jnp.float32
        ),
        "seq",
        scatter_dimension=0,
        tiled=True,
    )
    trunk_sum, unembed_sum = lax.psum((row_grad, weight_grad), "head")
    return (row_grad.astype(jnp.bfloat16)[None], trunk_sum.astype(jnp.bfloat16), unembed_sum)


def solution(mesh):
    in_specs = (
        P("seq", "mp"),
        P("head", "seq", "mp"),
        P("seq", "mp"),
        P("head", None),
        P("head", None),
    )
    out_specs = (P("head", "seq", "mp"), P("seq", "mp"), P("seq", "mp"))
    return jax.shard_map(shards, mesh=mesh, in_specs=in_specs, out_specs=out_specs, check_vma=False)
```

profile of v0, /device:TPU:0, one launch (start us, length us, event | category | flops | bytes accessed | tf_op | source)
XLA Modules:
  0.0 359.2 jit_solution(3892800967753359351)
XLA Ops:
  7.2 0.0 all-gather.2.cloned.1.call-start
  7.2 1.7 fusion.1
  8.9 0.0 all-gather.2.cloned.1.call-update
  8.9 0.0 all-reduce.4.cloned.1.call-start
  8.9 44.8 %all-gather.2.cloned.1.call-done = bf16[128,4096]{1,0:T(8,128)(2,1)} async-done(((bf16[16,4096]{1,0:T(8,128)(2,1)}), bf16[128,4096]{1,0:T(8,128)(2,1)}) %all-gather.2.cloned.1.call-update) | async-done | bytes 1048592 | tf_op jit(solution)/shard_map/all_gather | solution.py:12
  53.7 14.0 %convolution_bitcast_fusion = f32[2304,128]{0,1:T(8,128)} fusion(bf16[128,4096]{1,0:T(8,128)(2,1)} %all-gather.2.cloned.1.call-done, bf16[2304,4096]{1,0:T(8,128)(2,1)} %param.7), kind=kOutput, calls=%fused_computation | convolution fusion | flops 2415919104 | bytes 21102592 | tf_op jit(solution)/shard_map/dot_general | solution.py:15
  67.8 0.0 copy-start.2
  67.8 0.0 copy-start.3
  67.8 0.0 all-reduce.4.cloned.1.call-update
  67.8 0.0 reduce-scatter.2.cloned.1.call-start
  67.9 41.8 %all-reduce.4.cloned.1.call-done = f32[2304,128]{0,1:T(8,128)} async-done(((f32[2304,128]{0,1:T(8,128)}), f32[2304,128]{0,1:T(8,128)}) %all-reduce.4.cloned.1.call-update) | async-done | bytes 1179664 | tf_op jit(solution)/shard_map/psum | solution.py:14
  109.6 0.0 copy-start
  109.6 1.8 fusion
  111.4 21.4 %psum.29 = f32[128]{0:T(128)S(1)} all-reduce(f32[128]{0:T(128)S(1)} %fusion), channel_id=1, replica_groups=mesh['head'=2,'seq'=8,'mp'=2] {'seq'}, use_global_device_ids=true, to_apply=%region_2.0 | all-reduce | flops 128 | bytes 1024 | tf_op jit(solution)/shard_map/psum | solution.py:23
  132.7 0.0 copy-done.2
  132.7 0.0 copy-done.3
  132.7 0.0 copy-done
  132.7 10.8 %fusion.3 = f32[128,4096]{1,0:T(8,128)} fusion(bf16[2304,4096]{1,0:T(8,128)(2,1)} %param.7, f32[2304,128]{0,1:T(8,128)S(1)} %copy-done, s32[2304]{0:T(1024)S(1)} %iota_add_fusion, f32[128]{0:T(128)S(1)} %psum.29, f32[128]{0:T(128)S(1)} %bitcast.13, s32[128]{0:T(128)S(1)} %bitcast.15), kind=kOutput, calls=%fused_computation.10 | convolution fusion | flops 2419163136 | bytes 22161920 | tf_op jit(solution)/shard_map/dot_general | solution.py:32
  143.5 0.0 copy-start.1
  143.5 0.0 reduce-scatter.2.cloned.1.call-update
  143.6 0.0 all-reduce.6.cloned.1.call-start
  143.6 1.1 copy-done.1
  144.8 15.9 %fusion.2 = f32[2304,4096]{1,0:T(8,128)} fusion(bf16[128,4096]{1,0:T(8,128)(2,1)S(1)} %copy-done.1, f32[2304,128]{0,1:T(8,128)S(1)} %copy-done, s32[2304]{0:T(1024)S(1)} %iota_add_fusion, f32[128]{0:T(128)S(1)} %psum.29, f32[128]{0:T(128)S(1)} %bitcast.14, s32[128]{0:T(128)S(1)} %bitcast.16), kind=kOutput, calls=%fused_computation.9 | convolution fusion | flops 2419163136 | bytes 39987712 | tf_op jit(solution)/shard_map/dot_general | solution.py:30
  160.6 0.0 all-reduce.6.cloned.1.call-update
  160.7 47.7 %reduce-scatter.2.cloned.1.call-done = f32[16,4096]{1,0:T(8,128)} async-done(((f32[128,4096]{1,0:T(8,128)}), f32[16,4096]{1,0:T(8,128)}) %reduce-scatter.2.cloned.1.call-update) | async-done | bytes 262160 | tf_op jit(solution)/shard_map/reduce_scatter | solution.py:31
  208.4 1.6 convert_bitcast_fusion
  210.0 5.4 %all-reduce.7 = bf16[16,4096]{1,0:T(8,128)(2,1)} all-reduce(f32[16,4096]{1,0:T(8,128)} %reduce-scatter.2.cloned.1.call-done), channel_id=1, replica_groups=mesh['head'=2,'seq'=8,'mp'=2] {'head'}, use_global_device_ids=true, to_apply=%region_4.0 | all-reduce | flops 65536 | bytes 393216 | tf_op jit(solution)/shard_map/psum | solution.py:39
  215.4 110.0 %all-reduce.6.cloned.1.call-done = f32[2304,4096]{1,0:T(8,128)} async-done(((f32[2304,4096]{1,0:T(8,128)}), f32[2304,4096]{1,0:T(8,128)}) %all-reduce.6.cloned.1.call-update) | async-done | bytes 37748752 | tf_op jit(solution)/shard_map/psum | solution.py:39
  325.4 27.3 %copy.12 = f32[2304,4096]{1,0:T(8,128)} copy(f32[2304,4096]{1,0:T(8,128)} %all-reduce.6.cloned.1.call-done) | data formatting | bytes 75497472
  (1 shorter events, 0.0 us)
Async XLA Ops:
  7.2 46.5 %all-gather.2.cloned.1.call-start = ((), (), s32[]{:S(2)}) async-start(), calls=%async_computation.1 | async-start | bytes 1179648 | tf_op jit(solution)/shard_map/all_gather | solution.py:12
  8.9 100.7 %all-reduce.4.cloned.1.call-start = ((), (), s32[]{:S(2)}) async-start(), calls=%async_computation.2 | async-start | bytes 2359296 | tf_op jit(solution)/shard_map/psum | solution.py:14
  67.8 65.0 %copy-start.2 = (f32[1,128]{1,0:T(1,128)S(1)}, f32[1,128]{1,0:T(1,128)}, u32[]{:S(2)}) copy-start(f32[1,128]{1,0:T(1,128)} %param.9) | copy-start | bytes 1540
  67.8 65.0 %copy-start.3 = (s32[1,128]{1,0:T(1,128)S(1)}, s32[1,128]{1,0:T(1,128)}, u32[]{:S(2)}) copy-start(s32[1,128]{1,0:T(1,128)} %param.8) | copy-start | bytes 1540
  67.8 140.6 %reduce-scatter.2.cloned.1.call-start = ((), (), s32[]{:S(2)}) async-start(), calls=%async_computation.3 | async-start | bytes 2359296 | tf_op jit(solution)/shard_map/reduce_scatter | solution.py:31
  109.6 23.1 %copy-start = (f32[2304,128]{0,1:T(8,128)S(1)}, f32[2304,128]{0,1:T(8,128)}, u32[]{:S(2)}) copy-start(f32[2304,128]{0,1:T(8,128)} %all-reduce.4.cloned.1.call-done) | copy-start | bytes 3538948
  143.5 1.2 copy-start.1
  143.6 181.8 %all-reduce.6.cloned.1.call-start = ((), (), s32[]{:S(2)}) async-start(), calls=%async_computation.4 | async-start | bytes 75497472 | tf_op jit(solution)/shard_map/psum | solution.py:39
Sparse Core Ops, SparseCore 0:
  10.7 42.9 all-gather.1
  67.9 41.6 all-reduce.3
  143.7 64.6 reduce-scatter.1
  211.3 114.0 all-reduce.5
where the time goes:
time: 360 us; the launch traced here: 359 us
  waiting for transfers between devices  244 us (68%)
  matrix products  40.7 us (11%)
  local copies, waits for them, and re-layouts  28.4 us (8%)
  blocking collectives  26.8 us (7%)
  between operations  13.8 us (4%)
  other arithmetic  5.04 us (1%)
    psum x1, waiting for transfers between devices, shards(): trunk_sum, unembed_sum = lax.psum((row_grad, weight_grad), 'head')  110 us
    reduce_scatter x1, waiting for transfers between devices, shards(): lax.psum_scatter(lax.dot_general(grad_logits, unembed, (((0,), (0,)), (()...  47.7 us
    all_gather x1, waiting for transfers between devices, shards(): gathered = lax.all_gather(hidden, 'seq', axis=0, tiled=True)  44.8 us
    psum x1, waiting for transfers between devices, shards(): lax.psum(lax.dot_general(unembed, gathered, (((1,), (1,)), ((), ())), pre...  41.8 us
    unnamed x9, local copies, waits for them, and re-layouts  28.4 us
    psum x1, blocking collectives, shards(): totals = lax.psum(jnp.sum(exponent, axis=0), 'seq')  21.4 us
    dot_general x1, matrix products, shards(): jnp.dot(grad_logits, gathered, preferred_element_type=jnp.float32)  15.9 us
    dot_general x1, matrix products, shards(): lax.dot_general(unembed, gathered, (((1,), (1,)), ((), ())), preferred_el...  14 us
  transfers between devices with their start and end apart: 4, of which 4 were waited for; matrix products, arithmetic and copies ran while one was open for 5% of the time, Pallas kernels for 0%

commit v1 on v0

--- a/solution.py
+++ b/solution.py
@@ -9,7 +9,24 @@
 def shards(trunk, branch, unembed, targets, loss_grad):
     block_rows = unembed.shape[0]
     hidden = (trunk.astype(jnp.float32) + branch[0].astype(jnp.float32)).astype(jnp.bfloat16)
-    gathered = lax.all_gather(hidden, "seq", axis=0, tiled=True)
+    earlier = jax.lax.axis_size("seq")
+    val = jax.lax.axis_index("seq")
+    all_values, part_now, piece_out = (earlier, val, hidden.shape[0])
+    local_out, low = (hidden, 1)
+    while low < all_values:
+        local_out = jnp.concatenate(
+            [
+                local_out,
+                jax.lax.ppermute(
+                    local_out,
+                    "seq",
+                    perm=[(k0, (k0 - low) % all_values) for k0 in range(all_values)],
+                ),
+            ],
+            axis=0,
+        )
+        low = 2 * low
+    gathered = jnp.roll(local_out, shift=part_now * piece_out, axis=0)
     seq_index = lax.axis_index("seq")
     scores = lax.psum(
         lax.dot_general(

time: 360 us -> 358 us (level)
  starting transfers between devices: 0.16 us -> 8.36 us
  waiting for transfers between devices: 244 us -> 236 us
    all_gather x1 -> x0, waiting for transfers between devices: 44.8 us -> none  [shards(): gathered = lax.all_gather(hidden, 'seq', axis=0, tiled=True)]
    ppermute x0 -> x3, waiting for transfers between devices: none -> 32 us  [shards(): jax.lax.ppermute(local_out, 'seq', perm=[(k0, (k0 - low) % all_values) fo...]
    ppermute x0 -> x3, starting transfers between devices: none -> 8.24 us  [shards(): jax.lax.ppermute(local_out, 'seq', perm=[(k0, (k0 - low) % all_values) fo...]
    unnamed x9 -> x13, local copies, waits for them, and re-layouts: 28.4 us -> 27.4 us
  transfers between devices with their start and end apart: 4 -> 6, of which waited for: 4 -> 6; matrix products, arithmetic and copies ran while one was open for 5% -> 5% of each run, Pallas kernels for 0% -> 0%
where the time goes in v1:
time: 358 us; the launch traced here: 357 us
  waiting for transfers between devices  236 us (66%)
  matrix products  40.6 us (11%)
  local copies, waits for them, and re-layouts  27.4 us (8%)
  blocking collectives  26.8 us (7%)
  between operations  13.8 us (4%)
  starting transfers between devices  8.36 us (2%)
  other arithmetic  4.44 us (1%)
    psum x1, waiting for transfers between devices, shards(): trunk_sum, unembed_sum = lax.psum((row_grad, weight_grad), 'head')  110 us
    reduce_scatter x1, waiting for transfers between devices, shards(): lax.psum_scatter(lax.dot_general(grad_logits, unembed, (((0,), (0,)), (()...  48.6 us
    psum x1, waiting for transfers between devices, shards(): lax.psum(lax.dot_general(unembed, gathered, (((1,), (1,)), ((), ())), pre...  45 us
    ppermute x3, waiting for transfers between devices, shards(): jax.lax.ppermute(local_out, 'seq', perm=[(k0, (k0 - low) % all_values) fo...  32 us
    unnamed x13, local copies, waits for them, and re-layouts  27.4 us
    psum x1, blocking collectives, shards(): totals = lax.psum(jnp.sum(exponent, axis=0), 'seq')  21.4 us
    dot_general x1, matrix products, shards(): jnp.dot(grad_logits, gathered, preferred_element_type=jnp.float32)  16.1 us
    dot_general x1, matrix products, shards(): lax.dot_general(unembed, gathered, (((1,), (1,)), ((), ())), preferred_el...  13.7 us
  transfers between devices with their start and end apart: 6, of which 6 were waited for; matrix products, arithmetic and copies ran while one was open for 5% of the time, Pallas kernels for 0%

profile of v1, /device:TPU:0, one launch (start us, length us, event | category | flops | bytes accessed | tf_op | source)
XLA Modules:
  0.0 357.1 jit_solution(2494538091465745470)
XLA Ops:
  7.2 0.0 all-reduce.4.cloned.1.call-start
  7.2 1.0 constant_dynamic-update-slice_fusion.7
  8.2 6.1 %collective-permute-start = (bf16[16,4096]{1,0:T(8,128)(2,1)S(1)}, bf16[16,4096]{1,0:T(8,128)(2,1)S(1)}, u32[]{:S(2)}, u32[]{:S(2)}) collective-permute-start(bf16[16,4096]{1,0:T(8,128)(2,1)S(1)} %get-tuple-element.4), channel_id=1, source_target_pairs={{0,14},{2,0},{4,2},{6,4},{8,6},{10,8},{12,10},{14,12},{1,15},{3,1}... | collective-permute-start | bytes 393224 | tf_op jit(solution)/shard_map/ppermute | solution.py:20
  14.3 2.8 collective-permute-done
  17.1 1.6 collective-permute-start.1
  18.7 5.7 %collective-permute-done.1 = bf16[32,4096]{1,0:T(8,128)(2,1)S(1)} collective-permute-done((bf16[32,4096]{1,0:T(8,128)(2,1)S(1)}, bf16[32,4096]{1,0:T(8,128)(2,1)S(1)}, u32[]{:S(2)}, u32[]{:S(2)}) %collective-permute-start.1) | collective-permute-done | bytes 262176 | tf_op jit(solution)/shard_map/ppermute | solution.py:20
  24.4 0.6 collective-permute-start.2
  25.0 23.5 %collective-permute-done.2 = bf16[64,4096]{1,0:T(8,128)(2,1)S(1)} collective-permute-done((bf16[64,4096]{1,0:T(8,128)(2,1)S(1)}, bf16[64,4096]{1,0:T(8,128)(2,1)S(1)}, u32[]{:S(2)}, u32[]{:S(2)}) %collective-permute-start.2) | collective-permute-done | bytes 524320 | tf_op jit(solution)/shard_map/ppermute | solution.py:20
  48.7 13.7 %convolution_bitcast_fusion = f32[2304,128]{0,1:T(8,128)} fusion(bf16[2304,4096]{1,0:T(8,128)(2,1)} %param.7, bf16[256,4096]{1,0:T(8,128)(2,1)S(1)} %constant_dynamic-update-slice_fusion, s32[]{:T(128)S(6)} %select_n.14), kind=kOutput, calls=%fused_computation | convolution fusion | flops 2415919104 | bytes 21102596 | tf_op jit(solution)/shard_map/dot_general | solution.py:32
  62.4 0.0 copy-start.1
  62.4 0.0 copy-start.2
  62.4 0.0 all-reduce.4.cloned.1.call-update
  62.4 0.0 reduce-scatter.2.cloned.1.call-start
  62.5 45.0 %all-reduce.4.cloned.1.call-done = f32[2304,128]{0,1:T(8,128)} async-done(((f32[2304,128]{0,1:T(8,128)}), f32[2304,128]{0,1:T(8,128)}) %all-reduce.4.cloned.1.call-update) | async-done | bytes 1179664 | tf_op jit(solution)/shard_map/psum | solution.py:31
  107.5 0.0 copy-start
  107.5 1.8 fusion
  109.2 21.4 %psum.29 = f32[128]{0:T(128)S(1)} all-reduce(f32[128]{0:T(128)S(1)} %fusion), channel_id=1, replica_groups=mesh['head'=2,'seq'=8,'mp'=2] {'seq'}, use_global_device_ids=true, to_apply=%region_2.3 | all-reduce | flops 128 | bytes 1024 | tf_op jit(solution)/shard_map/psum | solution.py:40
  130.6 0.0 copy-done.1
  130.6 0.0 copy-done.2
  130.6 0.0 copy-done
  130.6 10.8 %fusion.7 = f32[128,4096]{1,0:T(8,128)} fusion(bf16[2304,4096]{1,0:T(8,128)(2,1)} %param.7, f32[2304,128]{0,1:T(8,128)S(1)} %copy-done, s32[2304]{0:T(1024)S(1)} %iota_add_fusion, f32[128]{0:T(128)S(1)} %psum.29, f32[128]{0:T(128)S(1)} %bitcast.12, s32[128]{0:T(128)S(1)} %bitcast.14), kind=kOutput, calls=%fused_computation.24 | convolution fusion | flops 2419163136 | bytes 22161920 | tf_op jit(solution)/shard_map/dot_general | solution.py:49
  141.4 0.0 reduce-scatter.2.cloned.1.call-update
  141.4 0.0 all-reduce.6.cloned.1.call-start
  141.5 16.1 %fusion.1 = f32[2304,4096]{1,0:T(8,128)} fusion(bf16[256,4096]{1,0:T(8,128)(2,1)S(1)} %constant_dynamic-update-slice_fusion, s32[]{:T(128)S(6)} %select_n.14, f32[2304,128]{0,1:T(8,128)S(1)} %copy-done, s32[2304]{0:T(1024)S(1)} %iota_add_fusion, f32[128]{0:T(128)S(1)} %psum.29, f32[128]{0:T(128)S(1)} %bitcast.13, s32[128]{0:T(128)S(1)} %bitcast.15), kind=kOutput, calls=%fused_computation.5 | convolution fusion | flops 2419163136 | bytes 39990788 | tf_op jit(solution)/shard_map/dot_general | solution.py:47
  157.5 0.0 all-reduce.6.cloned.1.call-update
  157.6 48.6 %reduce-scatter.2.cloned.1.call-done = f32[16,4096]{1,0:T(8,128)} async-done(((f32[128,4096]{1,0:T(8,128)}), f32[16,4096]{1,0:T(8,128)}) %reduce-scatter.2.cloned.1.call-update) | async-done | bytes 262160 | tf_op jit(solution)/shard_map/reduce_scatter | solution.py:48
  206.1 1.6 convert_bitcast_fusion
  207.7 5.4 %all-reduce.7 = bf16[16,4096]{1,0:T(8,128)(2,1)} all-reduce(f32[16,4096]{1,0:T(8,128)} %reduce-scatter.2.cloned.1.call-done), channel_id=1, replica_groups=mesh['head'=2,'seq'=8,'mp'=2] {'head'}, use_global_device_ids=true, to_apply=%region_4.5 | all-reduce | flops 65536 | bytes 393216 | tf_op jit(solution)/shard_map/psum | solution.py:56
  213.2 110.1 %all-reduce.6.cloned.1.call-done = f32[2304,4096]{1,0:T(8,128)} async-done(((f32[2304,4096]{1,0:T(8,128)}), f32[2304,4096]{1,0:T(8,128)}) %all-reduce.6.cloned.1.call-update) | async-done | bytes 37748752 | tf_op jit(solution)/shard_map/psum | solution.py:56
  323.3 27.3 %copy.19 = f32[2304,4096]{1,0:T(8,128)} copy(f32[2304,4096]{1,0:T(8,128)} %all-reduce.6.cloned.1.call-done) | data formatting | bytes 75497472
  (10 shorter events, 0.2 us)
Async XLA Ops:
  7.2 100.3 %all-reduce.4.cloned.1.call-start = ((), (), s32[]{:S(2)}) async-start(), calls=%async_computation.1 | async-start | bytes 2359296 | tf_op jit(solution)/shard_map/psum | solution.py:31
  8.2 8.8 %collective-permute-start = (bf16[16,4096]{1,0:T(8,128)(2,1)S(1)}, bf16[16,4096]{1,0:T(8,128)(2,1)S(1)}, u32[]{:S(2)}, u32[]{:S(2)}) collective-permute-start(bf16[16,4096]{1,0:T(8,128)(2,1)S(1)} %get-tuple-element.4), channel_id=1, source_target_pairs={{0,14},{2,0},{4,2},{6,4},{8,6},{10,8},{12,10},{14,12},{1,15},{3,1}... | collective-permute-start | bytes 393224 | tf_op jit(solution)/shard_map/ppermute | solution.py:20
  17.1 7.2 %collective-permute-start.1 = (bf16[32,4096]{1,0:T(8,128)(2,1)S(1)}, bf16[32,4096]{1,0:T(8,128)(2,1)S(1)}, u32[]{:S(2)}, u32[]{:S(2)}) collective-permute-start(bf16[32,4096]{1,0:T(8,128)(2,1)S(1)} %pad_maximum_fusion.1), channel_id=1, source_target_pairs={{0,12},{2,14},{4,0},{6,2},{8,4},{10,6},{12,8},{14,10},{1,13},{3,15... | collective-permute-start | bytes 786440 | tf_op jit(solution)/shard_map/ppermute | solution.py:20
  24.4 24.2 %collective-permute-start.2 = (bf16[64,4096]{1,0:T(8,128)(2,1)S(1)}, bf16[64,4096]{1,0:T(8,128)(2,1)S(1)}, u32[]{:S(2)}, u32[]{:S(2)}) collective-permute-start(bf16[64,4096]{1,0:T(8,128)(2,1)S(1)} %pad_maximum_fusion), channel_id=1, source_target_pairs={{0,8},{2,10},{4,12},{6,14},{8,0},{10,2},{12,4},{14,6},{1,9},{3,11}... | collective-permute-start | bytes 1572872 | tf_op jit(solution)/shard_map/ppermute | solution.py:20
  62.4 68.2 %copy-start.1 = (f32[1,128]{1,0:T(1,128)S(1)}, f32[1,128]{1,0:T(1,128)}, u32[]{:S(2)}) copy-start(f32[1,128]{1,0:T(1,128)} %param.9) | copy-start | bytes 1540
  62.4 68.2 %copy-start.2 = (s32[1,128]{1,0:T(1,128)S(1)}, s32[1,128]{1,0:T(1,128)}, u32[]{:S(2)}) copy-start(s32[1,128]{1,0:T(1,128)} %param.8) | copy-start | bytes 1540
  62.4 143.7 %reduce-scatter.2.cloned.1.call-start = ((), (), s32[]{:S(2)}) async-start(), calls=%async_computation.2 | async-start | bytes 2359296 | tf_op jit(solution)/shard_map/reduce_scatter | solution.py:48
  107.5 23.1 %copy-start = (f32[2304,128]{0,1:T(8,128)S(1)}, f32[2304,128]{0,1:T(8,128)}, u32[]{:S(2)}) copy-start(f32[2304,128]{0,1:T(8,128)} %all-reduce.4.cloned.1.call-done) | copy-start | bytes 3538948
  141.4 181.9 %all-reduce.6.cloned.1.call-start = ((), (), s32[]{:S(2)}) async-start(), calls=%async_computation.3 | async-start | bytes 75497472 | tf_op jit(solution)/shard_map/psum | solution.py:56
Sparse Core Ops, SparseCore 0:
  62.5 44.8 all-reduce.3
  141.5 64.5 reduce-scatter.1
  209.2 114.0 all-reduce.5
